TPU v7x, 32 devices: a whole 2x2x4 slice. The times are simulated.
32 devices in a mesh: wide: 8 (over z, core), narrow: 4 (over y, x).
Axes of the slice: x: 2, y: 2, z: 4, core: 2. Of those that a mesh axis runs over, the one named last changes fastest.
Arguments:
- offsets: float32 [2, 8, 4, 8192], P(None, 'wide', 'narrow'), may hold values from -1 to 1
- strengths: float32 [2, 8, 4, 8192], P(None, 'wide', 'narrow'), may hold values from -1.2 to 1.2
- leaf_map: int32 [8, 4, 8192], P('wide', 'narrow'), may hold values from 0 to 1023
- shift_matrices: float32 [7, 4, 128, 128], replicated, may hold values from -0.25 to 0.25
- transfer_diagonal: float32 [5, 49, 128], replicated, may hold values from -1.25 to 1.25
Outputs:
- leaf_multipoles: float32 [256, 128, 128], P('wide', 'narrow')
- local_zero: float32 [8, 4, 128], P('wide', 'narrow')
- local_one: float32 [16, 8, 128], P('wide', 'narrow')
- local_two: float32 [32, 16, 128], P('wide', 'narrow')
- local_three: float32 [64, 32, 128], P('wide', 'narrow')
- coarse_local: float32 [4, 2, 128], replicated
- top_multipole: float32 [2, 1, 128], replicated
All inputs are finite; a program needn't handle non-finite values.
Results may differ from a plain program's by a relative error of at most 0.0003.
Values sent between devices are 32-bit elements; how exact they have to be, the bound alone decides.
A program may use at most 128 MiB of HBM per device.

v0:
```python
import functools
import math

import jax
import jax.numpy as jnp
from jax import lax
from jax.experimental import pallas as pl
from jax.experimental.pallas import tpu as pltpu
from jax.sharding import PartitionSpec as P

F32 = jnp.float32
BF16 = jnp.bfloat16
MESH = pl.DeviceIdType.MESH
COARSE = 2
SIDE = 32
CHUNK = 4096


def split(x):
    hi = x.astype(BF16)
    return hi, (x - hi.astype(F32)).astype(BF16)


def dot(a, b):
    return jnp.dot(a, b, preferred_element_type=F32)


def halves(weight):
    return jnp.concatenate(split(weight), axis=1)


def merge(parts, weight):
    width = parts[0].shape[1]
    lhs = jnp.concatenate(parts, axis=1)
    hi, lo = split(lhs)
    both = dot(hi, weight)
    return both[:, :width] + (both[:, width:] + dot(lo, weight[:, :width]))


def cheb_start(a):
    k = lax.broadcasted_iota(jnp.int32, a.shape, 0)
    t = [jnp.ones_like(a), a]
    twice = a + a
    for _ in range(7):
        t.append(twice * t[-1] - t[-2])
    cur, prev = t[0], t[8]
    for n in range(1, 8):
        cur = jnp.where(k == n, t[n], cur)
        prev = jnp.where(k == n, t[8 - n], prev)
    return t[8] + t[8], prev, cur


def panel_sums(order, chunk, off_ref, str_ref, map_ref, leaf_ref, acc_ref):
    panels = off_ref.shape[-1]

    def add(i, first):
        at = pl.ds(pl.multiple_of(i * chunk, chunk), chunk)
        wide8 = lambda ref, n: jnp.broadcast_to(ref[n, 0, :, at], (8, chunk))
        a, b = wide8(off_ref, 0), wide8(off_ref, 1)
        qr, qi = wide8(str_ref, 0), wide8(str_ref, 1)
        ma, pa, ca = cheb_start(a)
        mb, pb, cb = cheb_start(b)
        real, imag = [], []
        for j in range(order // 8):
            real.append(qr * ca - qi * cb)
            imag.append(qr * cb + qi * ca)
            if j + 1 < order // 8:
                ca, pa = ma * ca - pa, ca
                cb, pb = mb * cb - pb, cb
        hi, lo = split(jnp.concatenate(real + imag, axis=0))
        terms = jnp.concatenate([hi, lo], axis=0)
        leaf = jnp.broadcast_to(map_ref[0, :, at], (SIDE, chunk))
        row = (leaf // SIDE).astype(F32).astype(BF16)
        col = leaf % SIDE
        one = (col == lax.broadcasted_iota(jnp.int32, (SIDE, chunk), 0)).astype(F32).astype(BF16)
        zero = jnp.zeros_like(one)
        sel = jnp.concatenate([jnp.where(row == r, one, zero) for r in range(SIDE)], axis=0)
        part = lax.dot_general(sel, terms, (((1,), (1,)), ((), ())), preferred_element_type=F32)
        acc_ref[...] = part if first else acc_ref[...] + part

    def body(i, carry):
        add(i, False)
        return carry

    add(0, True)
    lax.fori_loop(1, panels // chunk, body, 0)
    width = 2 * order
    leaf_ref[...] = acc_ref[:, :width] + acc_ref[:, width:]


def upward(shift_ref, leaf_ref, l3_ref, l2_ref):
    width = leaf_ref.shape[-1]

    def weight(level):
        return halves(shift_ref[COARSE + level].reshape(4 * width, width))

    parts = []
    for r0 in range(2):
        for c0 in range(2):
            rows = []
            for r1 in range(2):
                for c1 in range(2):
                    for top in range(8):
                        start = (4 * top + 2 * r1 + r0) * SIDE + 2 * c1 + c0
                        rows.append(leaf_ref[pl.ds(start, 8, stride=4), :])
            parts.append(jnp.concatenate(rows, axis=0))
    level4 = merge(parts, weight(4))
    level3 = merge([level4[64 * q : 64 * q + 64] for q in range(4)], weight(3))
    l3_ref[...] = level3
    parts = []
    for rb in range(2):
        for cb in range(2):
            parts.append(jnp.concatenate([l3_ref[pl.ds((2 * r + rb) * 8 + cb, 4, stride=2), :] for r in range(4)], axis=0))
    l2_ref[...] = merge(parts, weight(2))
    parts = []
    for rb in range(2):
        for cb in range(2):
            parts.append(jnp.concatenate([l2_ref[pl.ds((2 * r + rb) * 4 + cb, 2, stride=2), :] for r in range(2)], axis=0))
    level1 = merge(parts, weight(1))
    level0 = merge([level1[q : q + 1] for q in range(4)], weight(0))
    return level1, level0


NEAR = [(dr, dc) for dr in range(-3, 4) for dc in range(-3, 4) if max(abs(dr), abs(dc)) >= 2]
AROUND = [(dw, dv) for dw in (-1, 0, 1) for dv in (-1, 0, 1) if (dw, dv) != (0, 0)]


def allowed(d, parity):
    return -2 - parity <= d <= 3 - parity


def tree_kernel(
    rows, cols, chunk,
    off_ref, str_ref, map_ref, shift_in, diag_in,
    leaf_ref, zero_out, one_out, two_out, three_out, coarse_out, top_out,
    acc_ref, shift_ref, diag_ref, l3_ref, l2_ref, l1_ref, l0_ref, load_sem,
    packed, landed, big, win3, win2, win1, sh3, sh2, sh1, xr, xi, lhs, grid1, coarse_w,
    send_all, recv_all, send_near, recv_near,
):
    w, v = lax.axis_index("wide"), lax.axis_index("narrow")
    count = rows * cols
    width = diag_ref.shape[-1]
    half = width // 2

    to_w = [lax.rem(w + i, rows) for i in range(rows)]
    to_v = [lax.rem(v + j, cols) for j in range(cols)]
    from_w = [lax.rem(w + rows - i, rows) for i in range(rows)]
    from_v = [lax.rem(v + cols - j, cols) for j in range(cols)]
    others = [(i, j) for i in range(rows) for j in range(cols) if (i, j) != (0, 0)]

    barrier = pltpu.get_barrier_semaphore()
    for i, j in others:
        pl.semaphore_signal(barrier, inc=1, device_id=(to_w[i], to_v[j]), device_id_type=MESH)
    loads = [
        pltpu.make_async_copy(shift_in, shift_ref, load_sem.at[0]),
        pltpu.make_async_copy(diag_in, diag_ref, load_sem.at[1]),
    ]
    for load in loads:
        load.start()

    panel_sums(half, chunk, off_ref, str_ref, map_ref, leaf_ref, acc_ref)
    for load in loads:
        load.wait()
    level1, level0 = upward(shift_ref, leaf_ref, l3_ref, l2_ref)
    l0_ref[...] = level0
    l1_ref[...] = jnp.concatenate([level1, jnp.zeros((4, width), F32)], axis=0)

    edge = {-1: 0, 1: 1}
    for dw, dv in AROUND:
        at = (1 + dw) * 3 + 1 + dv
        one_at = 24 if 0 in (dw, dv) else 8
        packed[at, pl.ds(one_at, 8)] = l1_ref[...]
        if dv == 0:
            packed[at, pl.ds(0, 16)] = l3_ref[pl.ds(48 * edge[dw], 16)]
            packed[at, pl.ds(16, 8)] = l2_ref[pl.ds(8 * edge[dw], 8)]
        elif dw == 0:
            for k in range(2):
                packed[at, pl.ds(8 * k, 8)] = l3_ref[pl.ds(6 * edge[dv] + k, 8, stride=8)]
                packed[at, pl.ds(16 + 4 * k, 4)] = l2_ref[pl.ds(2 * edge[dv] + k, 4, stride=4)]
        else:
            for k in range(2):
                packed[at, pl.ds(2 * k, 2)] = l3_ref[pl.ds((6 * edge[dw] + k) * 8 + 6 * edge[dv], 2)]
                packed[at, pl.ds(4 + 2 * k, 2)] = l2_ref[pl.ds((2 * edge[dw] + k) * 4 + 2 * edge[dv], 2)]
    pl.semaphore_wait(barrier, count - 1)

    def inside(dw, dv):
        ok = jnp.bool_(True)
        if dw < 0:
            ok = w > 0
        if dw > 0:
            ok = w < rows - 1
        if dv < 0:
            ok = ok & (v > 0)
        if dv > 0:
            ok = ok & (v < cols - 1)
        return ok

    def near_copy(dw, dv):
        out_at, in_at = (1 + dw) * 3 + 1 + dv, (1 - dw) * 3 + 1 - dv
        n = 32 if 0 in (dw, dv) else 16
        return pltpu.make_async_remote_copy(
            src_ref=packed.at[out_at, pl.ds(0, n)], dst_ref=landed.at[in_at, pl.ds(0, n)],
            send_sem=send_near.at[in_at], recv_sem=recv_near.at[in_at],
            device_id=(w + dw, v + dv), device_id_type=MESH)

    def all_copy(i, j, source):
        return pltpu.make_async_remote_copy(
            src_ref=l0_ref, dst_ref=big.at[3 + source[0], 3 + source[1]],
            send_sem=send_all.at[i * cols + j], recv_sem=recv_all.at[i * cols + j],
            device_id=(to_w[i], to_v[j]), device_id_type=MESH)

    for i, j in others:
        all_copy(i, j, (w, v)).start()
    for dw, dv in AROUND:
        @pl.when(inside(dw, dv))
        def _():
            near_copy(dw, dv).start()

    for dw, dv in AROUND:
        @pl.when(jnp.logical_not(inside(dw, dv)))
        def _():
            landed[(1 + dw) * 3 + 1 + dv] = jnp.zeros((32, width), F32)
    for r in range(rows + 6):
        for c in range(cols + 6):
            if not (3 <= r < rows + 3 and 3 <= c < cols + 3):
                big[r, c] = jnp.zeros((1, width), F32)
    big[3 + w, 3 + v] = l0_ref[...]

    lane = lax.broadcasted_iota(jnp.int32, (diag_ref.shape[1], width), 1) < half
    for s in range(diag_ref.shape[0]):
        d = diag_ref[s]
        turned = pltpu.roll(d, half, 1)
        xr[s] = jnp.where(lane, d, turned)
        xi[s] = jnp.where(lane, turned, d)
    for t in range(COARSE):
        coarse_w[t] = halves(shift_ref[t].reshape(4 * width, width))
    sign = jnp.where(lax.broadcasted_iota(jnp.int32, (1, width), 1) < half, -1.0, 1.0).astype(F32)
    odd = lax.rem(lax.broadcasted_iota(jnp.int32, (8, width), 0), 2) == 1

    def col_mask(dc, slab):
        if dc == -3:
            return jnp.where(odd, slab, 0.0)
        if dc == 3:
            return jnp.where(odd, 0.0, slab)
        return slab

    def factor(s, dr, dc):
        at = pl.ds(7 * (dr + 3) + dc + 3, 1)
        return xr[s, at, :], xi[s, at, :]

    def finish(acc_r, acc_i):
        return acc_r + sign * pltpu.roll(acc_i, half, 1)

    for r in range(8):
        win3[pl.ds((2 + r) * 24 + 8, 8)] = l3_ref[pl.ds(8 * r, 8)]
    for r in range(4):
        win2[pl.ds((2 + r) * 16 + 4, 4)] = l2_ref[pl.ds(4 * r, 4)]
    for r in range(2):
        win1[pl.ds((2 + r) * 16 + 4, 2)] = l1_ref[pl.ds(2 * r, 2)]

    def near_level(s, n, window, pitch, shifted, out):
        left = 8 if n == 8 else 4
        for dc in range(-3, 4):
            for r in range(n + 4):
                shifted[dc + 3, r] = col_mask(dc, window[pl.ds(r * pitch + left + dc, 8)])
        acc_r = [jnp.zeros((8, width), F32) for _ in range(n)]
        acc_i = [jnp.zeros((8, width), F32) for _ in range(n)]
        for dr, dc in NEAR:
            f_r, f_i = factor(s, dr, dc)
            for r in range(n):
                if allowed(dr, r % 2):
                    src = shifted[dc + 3, 2 + r + dr]
                    acc_r[r] = acc_r[r] + f_r * src
                    acc_i[r] = acc_i[r] + f_i * src
        for r in range(n):
            out[r] = finish(acc_r[r], acc_i[r])[: out.shape[1]]

    for dw, dv in AROUND:
        @pl.when(inside(dw, dv))
        def _():
            near_copy(-dw, -dv).wait_recv()

    for dw, dv in AROUND:
        at = (1 + dw) * 3 + 1 + dv
        first = lambda d, n: {-1: 0, 0: 2, 1: n + 2}[d]
        column = lambda d, n, left: {-1: left - 2, 0: left, 1: left + n}[d]
        r3, r2, r1 = first(dw, 8), first(dw, 4), first(dw, 2)
        c3, c2, c1 = column(dv, 8, 8), column(dv, 4, 4), column(dv, 2, 4)
        one_at = 24 if 0 in (dw, dv) else 8
        for k in range(2):
            win1[pl.ds((r1 + k) * 16 + c1, 2)] = landed[at, pl.ds(one_at + 2 * k, 2)]
            if dv == 0:
                win3[pl.ds((r3 + k) * 24 + c3, 8)] = landed[at, pl.ds(8 * k, 8)]
                win2[pl.ds((r2 + k) * 16 + c2, 4)] = landed[at, pl.ds(16 + 4 * k, 4)]
            elif dw == 0:
                win3[pl.ds(r3 * 24 + c3 + k, 8, stride=24)] = landed[at, pl.ds(8 * k, 8)]
                win2[pl.ds(r2 * 16 + c2 + k, 4, stride=16)] = landed[at, pl.ds(16 + 4 * k, 4)]
            else:
                win3[pl.ds((r3 + k) * 24 + c3, 2)] = landed[at, pl.ds(2 * k, 2)]
                win2[pl.ds((r2 + k) * 16 + c2, 2)] = landed[at, pl.ds(4 + 2 * k, 2)]
    near_level(4, 8, win3, 24, sh3, three_out)
    near_level(3, 4, win2, 16, sh2, two_out)
    near_level(2, 2, win1, 16, sh1, one_out)

    for i, j in others:
        all_copy(i, j, (from_w[i], from_v[j])).wait_recv()

    half_r, half_c = rows // 2, cols // 2
    for r in range(rows):
        for c in range(cols):
            q = 2 * (r % 2) + c % 2
            lhs[pl.ds((r // 2) * half_c + c // 2, 1), pl.ds(q * width, width)] = big[3 + r, 3 + c]
    boxes = half_r * half_c

    coarse = merge([lhs[:boxes, pl.ds(q * width, width)] for q in range(4)], coarse_w[1])
    grid1[:boxes] = coarse
    quarter_c = half_c // 2
    for r in range(half_r):
        for c in range(half_c):
            q = 2 * (r % 2) + c % 2
            lhs[pl.ds((r // 2) * quarter_c + c // 2, 1), pl.ds(q * width, width)] = grid1[pl.ds(r * half_c + c, 1)]
    tops = (half_r // 2) * quarter_c
    top = merge([lhs[:tops, pl.ds(q * width, width)] for q in range(4)], coarse_w[0])
    for r in range(half_r // 2):
        top_out[r] = top[r * quarter_c : (r + 1) * quarter_c]

    odd_w, odd_v = lax.rem(w, 2), lax.rem(v, 2)
    keep = {
        ("r", -3): odd_w.astype(F32), ("r", 3): (1 - odd_w).astype(F32),
        ("c", -3): odd_v.astype(F32), ("c", 3): (1 - odd_v).astype(F32),
    }
    acc_r = jnp.zeros((1, width), F32)
    acc_i = jnp.zeros((1, width), F32)
    for dr, dc in NEAR:
        f_r, f_i = factor(1, dr, dc)
        src = big[3 + w + dr, 3 + v + dc]
        if abs(dr) == 3:
            src = src * keep["r", dr]
        if abs(dc) == 3:
            src = src * keep["c", dc]
        acc_r = acc_r + f_r * src
        acc_i = acc_i + f_i * src
    zero_out[0] = finish(acc_r, acc_i)

    for r in range(half_r):
        line = []
        for c in range(half_c):
            acc_r = jnp.zeros((1, width), F32)
            acc_i = jnp.zeros((1, width), F32)
            for dr, dc in NEAR:
                if allowed(dr, r % 2) and allowed(dc, c % 2) and 0 <= r + dr < half_r and 0 <= c + dc < half_c:
                    f_r, f_i = factor(0, dr, dc)
                    src = grid1[pl.ds((r + dr) * half_c + c + dc, 1)]
                    acc_r = acc_r + f_r * src
                    acc_i = acc_i + f_i * src
            line.append(finish(acc_r, acc_i))
        coarse_out[r] = jnp.concatenate(line, axis=0)

    for dw, dv in AROUND:
        @pl.when(inside(dw, dv))
        def _():
            near_copy(dw, dv).wait_send()

    for i, j in others:
        all_copy(i, j, (w, v)).wait_send()


def write_kernel(n, *refs):
    sem = refs[2 * n]
    copies = [pltpu.make_async_copy(refs[k], refs[n + k], sem.at[k]) for k in range(n)]
    for copy in copies:
        copy.start()
    for copy in copies:
        copy.wait()


def local(mesh_shape, offsets, strengths, leaf_map, shift_matrices, transfer_diagonal):
    rows, cols = mesh_shape
    width = shift_matrices.shape[-1]
    levels = transfer_diagonal.shape[0]
    vmem = pl.BlockSpec(memory_space=pltpu.VMEM)
    boxes = (rows // 2) * (cols // 2)
    pad8 = -(-boxes // 8) * 8
    dims = (
        (SIDE * SIDE, width), (1, 1, width), (2, 2, width), (4, 4, width), (8, 8, width),
        (rows // 2, cols // 2, width), (rows // 4, cols // 4, width),
    )
    any_space = pl.BlockSpec(memory_space=pl.ANY)
    held = pl.pallas_call(
        functools.partial(tree_kernel, rows, cols, math.gcd(CHUNK, offsets.shape[-1])),
        out_shape=tuple(pltpu.VMEM(d, F32) for d in dims),
        in_specs=[vmem, vmem, vmem, any_space, any_space],
        out_specs=(vmem,) * len(dims),
        scratch_shapes=[
            pltpu.VMEM((SIDE * SIDE, 2 * width), F32),
            pltpu.VMEM(shift_matrices.shape, F32),
            pltpu.VMEM(transfer_diagonal.shape, F32),
            pltpu.VMEM((64, width), F32),
            pltpu.VMEM((16, width), F32),
            pltpu.VMEM((8, width), F32),
            pltpu.VMEM((1, width), F32),
            pltpu.SemaphoreType.DMA((2,)),
            pltpu.VMEM((9, 32, width), F32),
            pltpu.VMEM((9, 32, width), F32),
            pltpu.VMEM((rows + 6, cols + 6, 1, width), F32),
            pltpu.VMEM((12 * 24, width), F32),
            pltpu.VMEM((8 * 16, width), F32),
            pltpu.VMEM((6 * 16, width), F32),
            pltpu.VMEM((7, 12, 8, width), F32),
            pltpu.VMEM((7, 8, 8, width), F32),
            pltpu.VMEM((7, 6, 8, width), F32),
            pltpu.VMEM((levels, 49, width), F32),
            pltpu.VMEM((levels, 49, width), F32),
            pltpu.VMEM((pad8, 4 * width), F32),
            pltpu.VMEM((pad8, width), F32),
            pltpu.VMEM((COARSE, 4 * width, 2 * width), BF16),
            pltpu.SemaphoreType.DMA((rows * cols,)),
            pltpu.SemaphoreType.DMA((rows * cols,)),
            pltpu.SemaphoreType.DMA((9,)),
            pltpu.SemaphoreType.DMA((9,)),
        ],
        compiler_params=pltpu.CompilerParams(collective_id=0, has_side_effects=True),
        name="tree",
    )(offsets, strengths, leaf_map, shift_matrices, transfer_diagonal)
    n = len(dims)
    outs = pl.pallas_call(
        functools.partial(write_kernel, n),
        out_shape=tuple(jax.ShapeDtypeStruct(d, F32) for d in dims),
        in_specs=[vmem] * n,
        out_specs=(any_space,) * n,
        scratch_shapes=[pltpu.SemaphoreType.DMA((n,))],
        name="write",
    )(*[pltpu.with_memory_space_constraint(x, pltpu.VMEM) for x in held])
    return (outs[0].reshape(SIDE, SIDE, width),) + tuple(outs[1:])


def solution(mesh):
    split_2 = P("wide", "narrow", None)
    in_specs = (P(None, "wide", "narrow", None), P(None, "wide", "narrow", None), split_2, P(), P())
    out_specs = (split_2,) * 5 + (P(), P())
    body = functools.partial(local, (mesh.shape["wide"], mesh.shape["narrow"]))
    return jax.shard_map(body, mesh=mesh, in_specs=in_specs, out_specs=out_specs, check_vma=False)
```

profile of v0, /device:TPU:0, one launch (start us, length us, event | category | flops | bytes accessed | tf_op | source)
XLA Modules:
  0.0 18.6 jit_solution(1028152020445756526)
XLA Ops:
  0.6 17.1 %tree.1 = (f32[1024,128]{1,0:T(8,128)S(1)}, f32[1,1,128]{2,1,0:T(1,128)S(1)}, f32[2,2,128]{2,1,0:T(2,128)S(1)}, f32[4,4,128]{2,1,0:T(4,128)S(1)}, f32[8,8,128]{2...) custom-call(f32[2,1,1,8192]{3,2,1,0:T(1,128)} %off_ref.1, f32[2,1,1,8192]{3,2,1,0:T(1,128)} %str_ref.1, ...), custom_call_target="tpu_custom_call" | custom-call | tf_op jit(solution)/shard_map/tree/pallas_call | solution.py:389
  17.7 0.9 %write.1 = (f32[1024,128]{1,0:T(8,128)}, f32[1,1,128]{2,1,0:T(1,128)}, f32[2,2,128]{2,1,0:T(2,128)}, f32[4,4,128]{2,1,0:T(4,128)}, f32[8,8,128]{2,1,0:T(8,128)},...) custom-call(f32[1024,128]{1,0:T(8,128)S(1)} %get-tuple-element.21.refs_0_, f32[1,1,128]{2,1,0:T(1,128)S(1)} %get-tuple-element.22.refs_1_, ...), custom_call_target="tpu_custom_call" | custom-call | tf_op jit(solution)/shard_map/write/pallas_call | solution.py:426
where the time goes:
time: 18.8 us; the launch traced here: 18.6 us
  Pallas kernels  18 us (96%)
  between operations  0.64 us (3%)
    pallas_call x1, Pallas kernels, local(): pl.pallas_call(functools.partial(tree_kernel, rows, cols, math.gcd(CHUNK,...  17.1 us
    pallas_call x1, Pallas kernels, local(): pl.pallas_call(functools.partial(write_kernel, n), out_shape=tuple((jax.S...  0.87 us

commit v1 on v0

--- a/solution.py
+++ b/solution.py
@@ -13,7 +13,11 @@
 MESH = pl.DeviceIdType.MESH
 COARSE = 2
 SIDE = 32
-CHUNK = 4096
+GROUP = 32
+PAD = 12
+LANES = 128
+F8 = jnp.float8_e4m3fn
+F8_TOP = 384.0 * 128.0
 
 
 def split(x):
@@ -30,36 +34,38 @@
 
 
 def merge(parts, weight):
-    width = parts[0].shape[1]
+    rows, width = parts[0].shape
     lhs = jnp.concatenate(parts, axis=1)
-    hi, lo = split(lhs)
-    both = dot(hi, weight)
-    return both[:, :width] + (both[:, width:] + dot(lo, weight[:, :width]))
-
-
-def cheb_start(a):
-    k = lax.broadcasted_iota(jnp.int32, a.shape, 0)
-    t = [jnp.ones_like(a), a]
-    twice = a + a
-    for _ in range(7):
-        t.append(twice * t[-1] - t[-2])
-    cur, prev = t[0], t[8]
-    for n in range(1, 8):
-        cur = jnp.where(k == n, t[n], cur)
-        prev = jnp.where(k == n, t[8 - n], prev)
-    return t[8] + t[8], prev, cur
-
-
-def panel_sums(order, chunk, off_ref, str_ref, map_ref, leaf_ref, acc_ref):
-    panels = off_ref.shape[-1]
-
-    def add(i, first):
-        at = pl.ds(pl.multiple_of(i * chunk, chunk), chunk)
-        wide8 = lambda ref, n: jnp.broadcast_to(ref[n, 0, :, at], (8, chunk))
-        a, b = wide8(off_ref, 0), wide8(off_ref, 1)
-        qr, qi = wide8(str_ref, 0), wide8(str_ref, 1)
-        ma, pa, ca = cheb_start(a)
-        mb, pb, cb = cheb_start(b)
+    hi = lhs.astype(BF16).astype(F32)
+    both = dot(jnp.concatenate([hi, lhs - hi], axis=0).astype(BF16), weight)
+    return both[:rows, :width] + (both[:rows, width:] + both[rows:, :width])
+
+
+def panel_sums(order, off_ref, str_ref, map_ref, leaf_ref, acc_hi, acc_lo, cheb, midway):
+    lines, lanes = map_ref.shape
+    pitch = lines + PAD
+    half = SIDE // 2
+    for x in range(2):
+        a = off_ref[x]
+        t = [jnp.ones_like(a), a]
+        twice = a + a
+        for _ in range(7):
+            t.append(twice * t[-1] - t[-2])
+        for k in range(8):
+            cheb[2 * x, pl.ds(k * pitch, lines), :] = t[k]
+            cheb[2 * x + 1, pl.ds(k * pitch, lines), :] = t[8 - k]
+    peak = jnp.max(jnp.maximum(jnp.abs(str_ref[0]), jnp.abs(str_ref[1])))
+    peak = jnp.maximum(peak, 1e-30)
+    up, down = F8_TOP / peak, peak * (1.0 / F8_TOP)
+    place = lax.broadcasted_iota(jnp.int32, (SIDE, lanes), 0)
+
+    def operands(g):
+        line = lambda ref, n: jnp.broadcast_to(ref[n, pl.ds(g, 1), :], (8, lanes))
+        eight = lambda n: cheb[n, pl.ds(g, 8, stride=pitch), :]
+        qr, qi = line(str_ref, 0), line(str_ref, 1)
+        ca, pa, cb, pb = eight(0), eight(1), eight(2), eight(3)
+        ma, mb = line(cheb, 1), line(cheb, 3)
+        ma, mb = ma + ma, mb + mb
         real, imag = [], []
         for j in range(order // 8):
             real.append(qr * ca - qi * cb)
@@ -67,32 +73,46 @@
             if j + 1 < order // 8:
                 ca, pa = ma * ca - pa, ca
                 cb, pb = mb * cb - pb, cb
-        hi, lo = split(jnp.concatenate(real + imag, axis=0))
-        terms = jnp.concatenate([hi, lo], axis=0)
-        leaf = jnp.broadcast_to(map_ref[0, :, at], (SIDE, chunk))
-        row = (leaf // SIDE).astype(F32).astype(BF16)
-        col = leaf % SIDE
-        one = (col == lax.broadcasted_iota(jnp.int32, (SIDE, chunk), 0)).astype(F32).astype(BF16)
+        terms = jnp.concatenate(real + imag, axis=0)
+        hi = terms.astype(BF16)
+        lo = ((terms - hi.astype(F32)) * up).astype(F8)
+        leaf = jnp.broadcast_to(map_ref[pl.ds(g, 1), :], (SIDE, lanes))
+        row = leaf // SIDE
+        lower = row >= half
+        row = jnp.where(lower, row - half, row).astype(F32).astype(BF16)
+        one = (leaf % SIDE == place).astype(F32).astype(BF16)
         zero = jnp.zeros_like(one)
-        sel = jnp.concatenate([jnp.where(row == r, one, zero) for r in range(SIDE)], axis=0)
-        part = lax.dot_general(sel, terms, (((1,), (1,)), ((), ())), preferred_element_type=F32)
-        acc_ref[...] = part if first else acc_ref[...] + part
-
-    def body(i, carry):
-        add(i, False)
-        return carry
-
-    add(0, True)
-    lax.fori_loop(1, panels // chunk, body, 0)
+        sel = jnp.concatenate([jnp.where(row == r, one, zero) for r in range(half)], axis=0)
+        wide = lambda m: jnp.broadcast_to(m, (2 * order, lanes))
+        in_lower = wide(lower[:1].astype(F32)).astype(BF16) == 1
+        none = jnp.zeros_like(hi)
+        hi = jnp.concatenate([jnp.where(in_lower, none, hi), jnp.where(in_lower, hi, none)], axis=0)
+        in_lower = wide(lower[:1])
+        none = jnp.zeros_like(lo)
+        lo = jnp.concatenate([jnp.where(in_lower, none, lo), jnp.where(in_lower, lo, none)], axis=0)
+        return sel, hi, lo
+
+    def product(a, b):
+        return lax.dot_general(a, b, (((1,), (1,)), ((), ())), preferred_element_type=F32)
+
+    group = math.gcd(GROUP, lines)
+    for start in range(0, lines, group):
+        sel, hi, lo = (jnp.concatenate(x, axis=1) for x in zip(*(operands(g) for g in range(start, start + group))))
+        part_hi, part_lo = product(sel, hi), product(sel.astype(F8), lo)
+        acc_hi[...] = part_hi if start == 0 else acc_hi[...] + part_hi
+        acc_lo[...] = part_lo if start == 0 else acc_lo[...] + part_lo
+        if start == 0:
+            midway()
     width = 2 * order
-    leaf_ref[...] = acc_ref[:, :width] + acc_ref[:, width:]
-
-
-def upward(shift_ref, leaf_ref, l3_ref, l2_ref):
-    width = leaf_ref.shape[-1]
-
+    boxes = half * SIDE
+    for k in range(2):
+        cols = pl.ds(k * width, width)
+        leaf_ref[pl.ds(k * boxes, boxes), :] = acc_hi[:, cols] + acc_lo[:, cols] * down
+
+
+def upward(w_ref, leaf_ref, l3_ref, l2_ref):
     def weight(level):
-        return halves(shift_ref[COARSE + level].reshape(4 * width, width))
+        return w_ref[COARSE + level]
 
     parts = []
     for r0 in range(2):
@@ -129,12 +149,23 @@
     return -2 - parity <= d <= 3 - parity
 
 
+def factor(xr, xi, s, dr, dc):
+    at = pl.ds(7 * (dr + 3) + dc + 3, 1)
+    return xr[s, at, :], xi[s, at, :]
+
+
+def finish(acc_r, acc_i):
+    half = acc_r.shape[1] // 2
+    sign = jnp.where(lax.broadcasted_iota(jnp.int32, (1, acc_r.shape[1]), 1) < half, -1.0, 1.0).astype(F32)
+    return acc_r + sign * pltpu.roll(acc_i, half, 1)
+
+
 def tree_kernel(
-    rows, cols, chunk,
-    off_ref, str_ref, map_ref, shift_in, diag_in,
-    leaf_ref, zero_out, one_out, two_out, three_out, coarse_out, top_out,
-    acc_ref, shift_ref, diag_ref, l3_ref, l2_ref, l1_ref, l0_ref, load_sem,
-    packed, landed, big, win3, win2, win1, sh3, sh2, sh1, xr, xi, lhs, grid1, coarse_w,
+    rows, cols,
+    off_in, str_in, map_in, shift_in, diag_in,
+    leaf_ref, one_out, two_out, three_out, big, xr, xi, w_ref,
+    off_ref, str_ref, map_ref, acc_hi, acc_lo, cheb, shift_ref, diag_ref, l3_ref, l2_ref, l1_ref, l0_ref, load_sem,
+    packed, landed, win3, win2, win1, sh3, sh2, sh1,
     send_all, recv_all, send_near, recv_near,
 ):
     w, v = lax.axis_index("wide"), lax.axis_index("narrow")
@@ -146,25 +177,43 @@
     to_v = [lax.rem(v + j, cols) for j in range(cols)]
     from_w = [lax.rem(w + rows - i, rows) for i in range(rows)]
     from_v = [lax.rem(v + cols - j, cols) for j in range(cols)]
-    others = [(i, j) for i in range(rows) for j in range(cols) if (i, j) != (0, 0)]
-
+    others = [(i % rows, j % cols) for i in (2, 1, *range(3, rows + 1)) for j in range(1, cols + 1)]
+    others.remove((0, 0))
+
+    loads = [
+        pltpu.make_async_copy(source, target, load_sem.at[k])
+        for k, (source, target) in enumerate([
+            (off_in, off_ref), (str_in, str_ref), (map_in, map_ref), (shift_in, shift_ref), (diag_in, diag_ref)])
+    ]
+    for load in loads:
+        load.start()
     barrier = pltpu.get_barrier_semaphore()
     for i, j in others:
         pl.semaphore_signal(barrier, inc=1, device_id=(to_w[i], to_v[j]), device_id_type=MESH)
-    loads = [
-        pltpu.make_async_copy(shift_in, shift_ref, load_sem.at[0]),
-        pltpu.make_async_copy(diag_in, diag_ref, load_sem.at[1]),
-    ]
-    for load in loads:
-        load.start()
-
-    panel_sums(half, chunk, off_ref, str_ref, map_ref, leaf_ref, acc_ref)
-    for load in loads:
+
+    def split_weights():
+        for load in loads[3:]:
+            load.wait()
+        for level in range(shift_ref.shape[0]):
+            w_ref[level] = halves(shift_ref[level].reshape(4 * width, width))
+
+    for load in loads[:3]:
         load.wait()
-    level1, level0 = upward(shift_ref, leaf_ref, l3_ref, l2_ref)
+    panel_sums(half, off_ref, str_ref, map_ref, leaf_ref, acc_hi, acc_lo, cheb, split_weights)
+    level1, level0 = upward(w_ref, leaf_ref, l3_ref, l2_ref)
     l0_ref[...] = level0
+    pl.semaphore_wait(barrier, count - 1)
+
+    def all_copy(i, j, source):
+        return pltpu.make_async_remote_copy(
+            src_ref=l0_ref, dst_ref=big.at[3 + source[0], 3 + source[1]],
+            send_sem=send_all.at[i * cols + j], recv_sem=recv_all.at[i * cols + j],
+            device_id=(to_w[i], to_v[j]), device_id_type=MESH)
+
+    for i, j in others:
+        all_copy(i, j, (w, v)).start()
+
     l1_ref[...] = jnp.concatenate([level1, jnp.zeros((4, width), F32)], axis=0)
-
     edge = {-1: 0, 1: 1}
     for dw, dv in AROUND:
         at = (1 + dw) * 3 + 1 + dv
@@ -181,8 +230,6 @@
             for k in range(2):
                 packed[at, pl.ds(2 * k, 2)] = l3_ref[pl.ds((6 * edge[dw] + k) * 8 + 6 * edge[dv], 2)]
                 packed[at, pl.ds(4 + 2 * k, 2)] = l2_ref[pl.ds((2 * edge[dw] + k) * 4 + 2 * edge[dv], 2)]
-    pl.semaphore_wait(barrier, count - 1)
-
     def inside(dw, dv):
         ok = jnp.bool_(True)
         if dw < 0:
@@ -203,14 +250,6 @@
             send_sem=send_near.at[in_at], recv_sem=recv_near.at[in_at],
             device_id=(w + dw, v + dv), device_id_type=MESH)
 
-    def all_copy(i, j, source):
-        return pltpu.make_async_remote_copy(
-            src_ref=l0_ref, dst_ref=big.at[3 + source[0], 3 + source[1]],
-            send_sem=send_all.at[i * cols + j], recv_sem=recv_all.at[i * cols + j],
-            device_id=(to_w[i], to_v[j]), device_id_type=MESH)
-
-    for i, j in others:
-        all_copy(i, j, (w, v)).start()
     for dw, dv in AROUND:
         @pl.when(inside(dw, dv))
         def _():
@@ -232,9 +271,6 @@
         turned = pltpu.roll(d, half, 1)
         xr[s] = jnp.where(lane, d, turned)
         xi[s] = jnp.where(lane, turned, d)
-    for t in range(COARSE):
-        coarse_w[t] = halves(shift_ref[t].reshape(4 * width, width))
-    sign = jnp.where(lax.broadcasted_iota(jnp.int32, (1, width), 1) < half, -1.0, 1.0).astype(F32)
     odd = lax.rem(lax.broadcasted_iota(jnp.int32, (8, width), 0), 2) == 1
 
     def col_mask(dc, slab):
@@ -243,13 +279,6 @@
         if dc == 3:
             return jnp.where(odd, 0.0, slab)
         return slab
-
-    def factor(s, dr, dc):
-        at = pl.ds(7 * (dr + 3) + dc + 3, 1)
-        return xr[s, at, :], xi[s, at, :]
-
-    def finish(acc_r, acc_i):
-        return acc_r + sign * pltpu.roll(acc_i, half, 1)
 
     for r in range(8):
         win3[pl.ds((2 + r) * 24 + 8, 8)] = l3_ref[pl.ds(8 * r, 8)]
@@ -266,7 +295,7 @@
         acc_r = [jnp.zeros((8, width), F32) for _ in range(n)]
         acc_i = [jnp.zeros((8, width), F32) for _ in range(n)]
         for dr, dc in NEAR:
-            f_r, f_i = factor(s, dr, dc)
+            f_r, f_i = factor(xr, xi, s, dr, dc)
             for r in range(n):
                 if allowed(dr, r % 2):
                     src = shifted[dc + 3, 2 + r + dr]
@@ -305,6 +334,31 @@
     for i, j in others:
         all_copy(i, j, (from_w[i], from_v[j])).wait_recv()
 
+    for dw, dv in AROUND:
+        @pl.when(inside(dw, dv))
+        def _():
+            near_copy(dw, dv).wait_send()
+
+    for i, j in others:
+        all_copy(i, j, (w, v)).wait_send()
+
+
+def last_kernel(
+    rows, cols,
+    leaf_ref, one_ref, two_ref, three_ref, big, xr, xi, w_ref,
+    leaf_hbm, zero_hbm, one_hbm, two_hbm, three_hbm, coarse_hbm, top_hbm,
+    zero_out, coarse_out, top_out, lhs, grid1, sem,
+):
+    w, v = lax.axis_index("wide"), lax.axis_index("narrow")
+    width = xr.shape[-1]
+    pairs = [
+        (leaf_ref, leaf_hbm), (one_ref, one_hbm), (two_ref, two_hbm), (three_ref, three_hbm),
+        (zero_out, zero_hbm), (coarse_out, coarse_hbm), (top_out, top_hbm),
+    ]
+    copies = [pltpu.make_async_copy(source, target, sem.at[k]) for k, (source, target) in enumerate(pairs)]
+    for copy in copies[:4]:
+        copy.start()
+
     half_r, half_c = rows // 2, cols // 2
     for r in range(rows):
         for c in range(cols):
@@ -312,7 +366,7 @@
             lhs[pl.ds((r // 2) * half_c + c // 2, 1), pl.ds(q * width, width)] = big[3 + r, 3 + c]
     boxes = half_r * half_c
 
-    coarse = merge([lhs[:boxes, pl.ds(q * width, width)] for q in range(4)], coarse_w[1])
+    coarse = merge([lhs[:boxes, pl.ds(q * width, width)] for q in range(4)], w_ref[1])
     grid1[:boxes] = coarse
     quarter_c = half_c // 2
     for r in range(half_r):
@@ -320,7 +374,7 @@
             q = 2 * (r % 2) + c % 2
             lhs[pl.ds((r // 2) * quarter_c + c // 2, 1), pl.ds(q * width, width)] = grid1[pl.ds(r * half_c + c, 1)]
     tops = (half_r // 2) * quarter_c
-    top = merge([lhs[:tops, pl.ds(q * width, width)] for q in range(4)], coarse_w[0])
+    top = merge([lhs[:tops, pl.ds(q * width, width)] for q in range(4)], w_ref[0])
     for r in range(half_r // 2):
         top_out[r] = top[r * quarter_c : (r + 1) * quarter_c]
 
@@ -332,7 +386,7 @@
     acc_r = jnp.zeros((1, width), F32)
     acc_i = jnp.zeros((1, width), F32)
     for dr, dc in NEAR:
-        f_r, f_i = factor(1, dr, dc)
+        f_r, f_i = factor(xr, xi, 1, dr, dc)
         src = big[3 + w + dr, 3 + v + dc]
         if abs(dr) == 3:
             src = src * keep["r", dr]
@@ -349,26 +403,14 @@
             acc_i = jnp.zeros((1, width), F32)
             for dr, dc in NEAR:
                 if allowed(dr, r % 2) and allowed(dc, c % 2) and 0 <= r + dr < half_r and 0 <= c + dc < half_c:
-                    f_r, f_i = factor(0, dr, dc)
+                    f_r, f_i = factor(xr, xi, 0, dr, dc)
                     src = grid1[pl.ds((r + dr) * half_c + c + dc, 1)]
                     acc_r = acc_r + f_r * src
                     acc_i = acc_i + f_i * src
             line.append(finish(acc_r, acc_i))
         coarse_out[r] = jnp.concatenate(line, axis=0)
 
-    for dw, dv in AROUND:
-        @pl.when(inside(dw, dv))
-        def _():
-            near_copy(dw, dv).wait_send()
-
-    for i, j in others:
-        all_copy(i, j, (w, v)).wait_send()
-
-
-def write_kernel(n, *refs):
-    sem = refs[2 * n]
-    copies = [pltpu.make_async_copy(refs[k], refs[n + k], sem.at[k]) for k in range(n)]
-    for copy in copies:
+    for copy in copies[4:]:
         copy.start()
     for copy in copies:
         copy.wait()
@@ -377,43 +419,46 @@
 def local(mesh_shape, offsets, strengths, leaf_map, shift_matrices, transfer_diagonal):
     rows, cols = mesh_shape
     width = shift_matrices.shape[-1]
-    levels = transfer_diagonal.shape[0]
+    levels, spots = transfer_diagonal.shape[:2]
+    depth = shift_matrices.shape[0]
+    panels = offsets.shape[-1]
+    lines = panels // LANES
     vmem = pl.BlockSpec(memory_space=pltpu.VMEM)
+    any_space = pl.BlockSpec(memory_space=pl.ANY)
     boxes = (rows // 2) * (cols // 2)
     pad8 = -(-boxes // 8) * 8
-    dims = (
-        (SIDE * SIDE, width), (1, 1, width), (2, 2, width), (4, 4, width), (8, 8, width),
-        (rows // 2, cols // 2, width), (rows // 4, cols // 4, width),
+    held_dims = (
+        ((SIDE * SIDE, width), F32), ((2, 2, width), F32), ((4, 4, width), F32), ((8, 8, width), F32),
+        ((rows + 6, cols + 6, 1, width), F32), ((levels, spots, width), F32), ((levels, spots, width), F32),
+        ((depth, 4 * width, 2 * width), BF16),
     )
-    any_space = pl.BlockSpec(memory_space=pl.ANY)
     held = pl.pallas_call(
-        functools.partial(tree_kernel, rows, cols, math.gcd(CHUNK, offsets.shape[-1])),
-        out_shape=tuple(pltpu.VMEM(d, F32) for d in dims),
-        in_specs=[vmem, vmem, vmem, any_space, any_space],
-        out_specs=(vmem,) * len(dims),
+        functools.partial(tree_kernel, rows, cols),
+        out_shape=tuple(pltpu.VMEM(*d) for d in held_dims),
+        in_specs=[any_space] * 5,
+        out_specs=(vmem,) * len(held_dims),
         scratch_shapes=[
-            pltpu.VMEM((SIDE * SIDE, 2 * width), F32),
+            pltpu.VMEM((2, lines, LANES), F32),
+            pltpu.VMEM((2, lines, LANES), F32),
+            pltpu.VMEM((lines, LANES), jnp.int32),
+            pltpu.VMEM((SIDE * SIDE // 2, 2 * width), F32),
+            pltpu.VMEM((SIDE * SIDE // 2, 2 * width), F32),
+            pltpu.VMEM((4, 8 * (lines + PAD), LANES), F32),
             pltpu.VMEM(shift_matrices.shape, F32),
             pltpu.VMEM(transfer_diagonal.shape, F32),
             pltpu.VMEM((64, width), F32),
             pltpu.VMEM((16, width), F32),
             pltpu.VMEM((8, width), F32),
             pltpu.VMEM((1, width), F32),
-            pltpu.SemaphoreType.DMA((2,)),
+            pltpu.SemaphoreType.DMA((5,)),
             pltpu.VMEM((9, 32, width), F32),
             pltpu.VMEM((9, 32, width), F32),
-            pltpu.VMEM((rows + 6, cols + 6, 1, width), F32),
             pltpu.VMEM((12 * 24, width), F32),
             pltpu.VMEM((8 * 16, width), F32),
             pltpu.VMEM((6 * 16, width), F32),
             pltpu.VMEM((7, 12, 8, width), F32),
             pltpu.VMEM((7, 8, 8, width), F32),
             pltpu.VMEM((7, 6, 8, width), F32),
-            pltpu.VMEM((levels, 49, width), F32),
-            pltpu.VMEM((levels, 49, width), F32),
-            pltpu.VMEM((pad8, 4 * width), F32),
-            pltpu.VMEM((pad8, width), F32),
-            pltpu.VMEM((COARSE, 4 * width, 2 * width), BF16),
             pltpu.SemaphoreType.DMA((rows * cols,)),
             pltpu.SemaphoreType.DMA((rows * cols,)),
             pltpu.SemaphoreType.DMA((9,)),
@@ -421,15 +466,28 @@
         ],
         compiler_params=pltpu.CompilerParams(collective_id=0, has_side_effects=True),
         name="tree",
-    )(offsets, strengths, leaf_map, shift_matrices, transfer_diagonal)
-    n = len(dims)
+    )(
+        offsets.reshape(2, lines, LANES), strengths.reshape(2, lines, LANES), leaf_map.reshape(lines, LANES),
+        shift_matrices, transfer_diagonal,
+    )
+    dims = (
+        (SIDE * SIDE, width), (1, 1, width), (2, 2, width), (4, 4, width), (8, 8, width),
+        (rows // 2, cols // 2, width), (rows // 4, cols // 4, width),
+    )
     outs = pl.pallas_call(
-        functools.partial(write_kernel, n),
+        functools.partial(last_kernel, rows, cols),
         out_shape=tuple(jax.ShapeDtypeStruct(d, F32) for d in dims),
-        in_specs=[vmem] * n,
-        out_specs=(any_space,) * n,
-        scratch_shapes=[pltpu.SemaphoreType.DMA((n,))],
-        name="write",
+        in_specs=[vmem] * len(held),
+        out_specs=(any_space,) * len(dims),
+        scratch_shapes=[
+            pltpu.VMEM(dims[1], F32),
+            pltpu.VMEM(dims[5], F32),
+            pltpu.VMEM(dims[6], F32),
+            pltpu.VMEM((pad8, 4 * width), F32),
+            pltpu.VMEM((pad8, width), F32),
+            pltpu.SemaphoreType.DMA((len(dims),)),
+        ],
+        name="last",
     )(*[pltpu.with_memory_space_constraint(x, pltpu.VMEM) for x in held])
     return (outs[0].reshape(SIDE, SIDE, width),) + tuple(outs[1:])
 

time: 18.8 us -> 17.7 us (0.941)
  Pallas kernels: 18 us -> 16.9 us
    pallas_call x2, Pallas kernels: 18 us -> 16.9 us  [the longest x1 15.9 us: local(): pl.pallas_call(functools.partial(tree_kernel, rows, cols), out_shape=tupl...]
where the time goes in v1:
time: 17.7 us; the launch traced here: 17.5 us
  Pallas kernels  16.9 us (95%)
  between operations  0.64 us (4%)
    pallas_call x1, Pallas kernels, local(): pl.pallas_call(functools.partial(tree_kernel, rows, cols), out_shape=tupl...  15.9 us
    pallas_call x1, Pallas kernels, local(): pl.pallas_call(functools.partial(last_kernel, rows, cols), out_shape=tupl...  0.92 us

profile of v1, /device:TPU:0, one launch (start us, length us, event | category | flops | bytes accessed | tf_op | source)
XLA Modules:
  0.0 17.5 jit_solution(5240431078880682417)
XLA Ops:
  0.6 15.9 %tree.1 = (f32[1024,128]{1,0:T(8,128)S(1)}, f32[2,2,128]{2,1,0:T(2,128)S(1)}, f32[4,4,128]{2,1,0:T(4,128)S(1)}, f32[8,8,128]{2,1,0:T(8,128)S(1)}, f32[14,10,1,12...) custom-call(f32[2,64,128]{2,1,0:T(8,128)} %bitcast.4, ...), custom_call_target="tpu_custom_call" | custom-call | tf_op jit(solution)/shard_map/tree/pallas_call | solution.py:435
  16.6 0.9 %last.1 = (f32[1024,128]{1,0:T(8,128)}, f32[1,1,128]{2,1,0:T(1,128)}, f32[2,2,128]{2,1,0:T(2,128)}, f32[4,4,128]{2,1,0:T(4,128)}, f32[8,8,128]{2,1,0:T(8,128)}, ...) custom-call(f32[1024,128]{1,0:T(8,128)S(1)} %get-tuple-element.22.leaf_ref, f32[2,2,128]{2,1,0:T(2,128)S(1)} %get-tuple-element.23.one_ref, ...), custom_call_target="tpu_custom_call" | custom-call | tf_op jit(solution)/shard_map/last/pallas_call | solution.py:477

commit v2 on v1

--- a/solution.py
+++ b/solution.py
@@ -1,5 +1,4 @@
 import functools
-import math
 
 import jax
 import jax.numpy as jnp
@@ -13,7 +12,6 @@
 MESH = pl.DeviceIdType.MESH
 COARSE = 2
 SIDE = 32
-GROUP = 32
 PAD = 12
 LANES = 128
 F8 = jnp.float8_e4m3fn
@@ -41,7 +39,7 @@
     return both[:rows, :width] + (both[:rows, width:] + both[rows:, :width])
 
 
-def panel_sums(order, off_ref, str_ref, map_ref, leaf_ref, acc_hi, acc_lo, cheb, midway):
+def panel_sums(order, off_ref, str_ref, map_ref, leaf_ref, cheb):
     lines, lanes = map_ref.shape
     pitch = lines + PAD
     half = SIDE // 2
@@ -74,8 +72,7 @@
                 ca, pa = ma * ca - pa, ca
                 cb, pb = mb * cb - pb, cb
         terms = jnp.concatenate(real + imag, axis=0)
-        hi = terms.astype(BF16)
-        lo = ((terms - hi.astype(F32)) * up).astype(F8)
+        high = terms.astype(BF16)
         leaf = jnp.broadcast_to(map_ref[pl.ds(g, 1), :], (SIDE, lanes))
         row = leaf // SIDE
         lower = row >= half
@@ -83,31 +80,38 @@
         one = (leaf % SIDE == place).astype(F32).astype(BF16)
         zero = jnp.zeros_like(one)
         sel = jnp.concatenate([jnp.where(row == r, one, zero) for r in range(half)], axis=0)
-        wide = lambda m: jnp.broadcast_to(m, (2 * order, lanes))
-        in_lower = wide(lower[:1].astype(F32)).astype(BF16) == 1
-        none = jnp.zeros_like(hi)
-        hi = jnp.concatenate([jnp.where(in_lower, none, hi), jnp.where(in_lower, hi, none)], axis=0)
-        in_lower = wide(lower[:1])
+        in_lower = jnp.broadcast_to(lower[:1].astype(F32), high.shape).astype(BF16) == 1
+        none = jnp.zeros_like(high)
+        hi = jnp.concatenate([jnp.where(in_lower, none, high), jnp.where(in_lower, high, none)], axis=0)
+        return sel, hi, (terms, high, lower[:1])
+
+    def low_operand(terms, high, lower, factor):
+        lo = ((terms - high.astype(F32)) * factor).astype(F8)
+        in_lower = jnp.broadcast_to(lower, lo.shape)
         none = jnp.zeros_like(lo)
-        lo = jnp.concatenate([jnp.where(in_lower, none, lo), jnp.where(in_lower, lo, none)], axis=0)
-        return sel, hi, lo
+        return jnp.concatenate([jnp.where(in_lower, none, lo), jnp.where(in_lower, lo, none)], axis=0)
 
     def product(a, b):
         return lax.dot_general(a, b, (((1,), (1,)), ((), ())), preferred_element_type=F32)
 
-    group = math.gcd(GROUP, lines)
-    for start in range(0, lines, group):
-        sel, hi, lo = (jnp.concatenate(x, axis=1) for x in zip(*(operands(g) for g in range(start, start + group))))
-        part_hi, part_lo = product(sel, hi), product(sel.astype(F8), lo)
-        acc_hi[...] = part_hi if start == 0 else acc_hi[...] + part_hi
-        acc_lo[...] = part_lo if start == 0 else acc_lo[...] + part_lo
-        if start == 0:
-            midway()
+    sels, his, rests = zip(*(operands(g) for g in range(lines)))
     width = 2 * order
     boxes = half * SIDE
-    for k in range(2):
-        cols = pl.ds(k * width, width)
-        leaf_ref[pl.ds(k * boxes, boxes), :] = acc_hi[:, cols] + acc_lo[:, cols] * down
+    step = boxes // 2
+    early = lines // 16
+    join = lambda x: jnp.concatenate(x, axis=1)
+    part_hi = []
+    for some in (slice(early), slice(early, lines)):
+        sel, hi = join(sels[some]), join(his[some])
+        part_hi.append([product(sel[step * m : step * m + step], hi) for m in range(2)])
+    up = up + part_hi[0][0][:1, :width] * 0.0
+    sel = join(sels).astype(F8)
+    lo = join([low_operand(*rest, up) for rest in rests])
+    part_lo = [product(sel[step * m : step * m + step], lo) for m in range(2)]
+    for m in range(2):
+        both = part_hi[0][m] + part_hi[1][m] + part_lo[m] * down
+        for k in range(2):
+            leaf_ref[pl.ds(k * boxes + m * step, step), :] = both[:, k * width : k * width + width]
 
 
 def upward(w_ref, leaf_ref, l3_ref, l2_ref):
@@ -164,7 +168,7 @@
     rows, cols,
     off_in, str_in, map_in, shift_in, diag_in,
     leaf_ref, one_out, two_out, three_out, big, xr, xi, w_ref,
-    off_ref, str_ref, map_ref, acc_hi, acc_lo, cheb, shift_ref, diag_ref, l3_ref, l2_ref, l1_ref, l0_ref, load_sem,
+    off_ref, str_ref, map_ref, cheb, shift_ref, diag_ref, l3_ref, l2_ref, l1_ref, l0_ref, load_sem,
     packed, landed, win3, win2, win1, sh3, sh2, sh1,
     send_all, recv_all, send_near, recv_near,
 ):
@@ -191,15 +195,13 @@
     for i, j in others:
         pl.semaphore_signal(barrier, inc=1, device_id=(to_w[i], to_v[j]), device_id_type=MESH)
 
-    def split_weights():
-        for load in loads[3:]:
-            load.wait()
-        for level in range(shift_ref.shape[0]):
-            w_ref[level] = halves(shift_ref[level].reshape(4 * width, width))
-
     for load in loads[:3]:
         load.wait()
-    panel_sums(half, off_ref, str_ref, map_ref, leaf_ref, acc_hi, acc_lo, cheb, split_weights)
+    panel_sums(half, off_ref, str_ref, map_ref, leaf_ref, cheb)
+    for load in loads[3:]:
+        load.wait()
+    for level in range(shift_ref.shape[0]):
+        w_ref[level] = halves(shift_ref[level].reshape(4 * width, width))
     level1, level0 = upward(w_ref, leaf_ref, l3_ref, l2_ref)
     l0_ref[...] = level0
     pl.semaphore_wait(barrier, count - 1)
@@ -441,8 +443,6 @@
             pltpu.VMEM((2, lines, LANES), F32),
             pltpu.VMEM((2, lines, LANES), F32),
             pltpu.VMEM((lines, LANES), jnp.int32),
-            pltpu.VMEM((SIDE * SIDE // 2, 2 * width), F32),
-            pltpu.VMEM((SIDE * SIDE // 2, 2 * width), F32),
             pltpu.VMEM((4, 8 * (lines + PAD), LANES), F32),
             pltpu.VMEM(shift_matrices.shape, F32),
             pltpu.VMEM(transfer_diagonal.shape, F32),

time: 17.7 us -> 16.8 us (0.949)
  Pallas kernels: 16.9 us -> 16 us
    pallas_call x1, Pallas kernels: 15.9 us -> 15.1 us  [local(): pl.pallas_call(functools.partial(tree_kernel, rows, cols), out_shape=tupl...]
where the time goes in v2:
time: 16.8 us; the launch traced here: 16.6 us
  Pallas kernels  16 us (95%)
  between operations  0.64 us (4%)
    pallas_call x1, Pallas kernels, local(): pl.pallas_call(functools.partial(tree_kernel, rows, cols), out_shape=tupl...  15.1 us
    pallas_call x1, Pallas kernels, local(): pl.pallas_call(functools.partial(last_kernel, rows, cols), out_shape=tupl...  0.92 us

profile of v2, /device:TPU:0, one launch (start us, length us, event | category | flops | bytes accessed | tf_op | source)
XLA Modules:
  0.0 16.6 jit_solution(10155885178946934657)
XLA Ops:
  0.6 15.1 %tree.1 = (f32[1024,128]{1,0:T(8,128)S(1)}, f32[2,2,128]{2,1,0:T(2,128)S(1)}, f32[4,4,128]{2,1,0:T(4,128)S(1)}, f32[8,8,128]{2,1,0:T(8,128)S(1)}, f32[14,10,1,12...) custom-call(f32[2,64,128]{2,1,0:T(8,128)} %bitcast.4, ...), custom_call_target="tpu_custom_call" | custom-call | tf_op jit(solution)/shard_map/tree/pallas_call | solution.py:437
  15.7 0.9 %last.1 = (f32[1024,128]{1,0:T(8,128)}, f32[1,1,128]{2,1,0:T(1,128)}, f32[2,2,128]{2,1,0:T(2,128)}, f32[4,4,128]{2,1,0:T(4,128)}, f32[8,8,128]{2,1,0:T(8,128)}, ...) custom-call(f32[1024,128]{1,0:T(8,128)S(1)} %get-tuple-element.22.leaf_ref, f32[2,2,128]{2,1,0:T(2,128)S(1)} %get-tuple-element.23.one_ref, ...), custom_call_target="tpu_custom_call" | custom-call | tf_op jit(solution)/shard_map/last/pallas_call | solution.py:477

commit v3 on v2

--- a/solution.py
+++ b/solution.py
@@ -28,18 +28,21 @@
 
 
 def halves(weight):
-    return jnp.concatenate(split(weight), axis=1)
+    cut = weight.shape[0] // 2
+    return jnp.concatenate(split(jnp.concatenate([weight[:cut], weight[cut:] * 2.0], axis=0)), axis=1)
 
 
 def merge(parts, weight):
     rows, width = parts[0].shape
     lhs = jnp.concatenate(parts, axis=1)
     hi = lhs.astype(BF16).astype(F32)
-    both = dot(jnp.concatenate([hi, lhs - hi], axis=0).astype(BF16), weight)
+    lhs = jnp.concatenate([hi, lhs - hi], axis=0).astype(BF16)
+    cut = 2 * width
+    both = dot(lhs[:, :cut], weight[:cut]) + dot(lhs[:, cut:], weight[cut:]) * 0.5
     return both[:rows, :width] + (both[:rows, width:] + both[rows:, :width])
 
 
-def panel_sums(order, off_ref, str_ref, map_ref, leaf_ref, cheb):
+def panel_sums(order, off_ref, str_ref, map_ref, leaf_ref, cheb, between):
     lines, lanes = map_ref.shape
     pitch = lines + PAD
     half = SIDE // 2
@@ -98,12 +101,13 @@
     width = 2 * order
     boxes = half * SIDE
     step = boxes // 2
-    early = lines // 16
+    early = lines // 32
     join = lambda x: jnp.concatenate(x, axis=1)
     part_hi = []
     for some in (slice(early), slice(early, lines)):
         sel, hi = join(sels[some]), join(his[some])
         part_hi.append([product(sel[step * m : step * m + step], hi) for m in range(2)])
+    between()
     up = up + part_hi[0][0][:1, :width] * 0.0
     sel = join(sels).astype(F8)
     lo = join([low_operand(*rest, up) for rest in rests])
@@ -128,7 +132,7 @@
                         start = (4 * top + 2 * r1 + r0) * SIDE + 2 * c1 + c0
                         rows.append(leaf_ref[pl.ds(start, 8, stride=4), :])
             parts.append(jnp.concatenate(rows, axis=0))
-    level4 = merge(parts, weight(4))
+    level4 = jnp.concatenate([merge([p[128 * m : 128 * m + 128] for p in parts], weight(4)) for m in range(2)], axis=0)
     level3 = merge([level4[64 * q : 64 * q + 64] for q in range(4)], weight(3))
     l3_ref[...] = level3
     parts = []
@@ -197,11 +201,14 @@
 
     for load in loads[:3]:
         load.wait()
-    panel_sums(half, off_ref, str_ref, map_ref, leaf_ref, cheb)
-    for load in loads[3:]:
-        load.wait()
-    for level in range(shift_ref.shape[0]):
-        w_ref[level] = halves(shift_ref[level].reshape(4 * width, width))
+
+    def split_weights():
+        for load in loads[3:]:
+            load.wait()
+        for level in range(shift_ref.shape[0]):
+            w_ref[level] = halves(shift_ref[level].reshape(4 * width, width))
+
+    panel_sums(half, off_ref, str_ref, map_ref, leaf_ref, cheb, split_weights)
     level1, level0 = upward(w_ref, leaf_ref, l3_ref, l2_ref)
     l0_ref[...] = level0
     pl.semaphore_wait(barrier, count - 1)
@@ -333,9 +340,6 @@
     near_level(3, 4, win2, 16, sh2, two_out)
     near_level(2, 2, win1, 16, sh1, one_out)
 
-    for i, j in others:
-        all_copy(i, j, (from_w[i], from_v[j])).wait_recv()
-
     for dw, dv in AROUND:
         @pl.when(inside(dw, dv))
         def _():
@@ -343,6 +347,8 @@
 
     for i, j in others:
         all_copy(i, j, (w, v)).wait_send()
+    for i, j in reversed(others):
+        all_copy(i, j, (from_w[i], from_v[j])).wait_recv()
 
 
 def last_kernel(

time: 16.8 us -> 16.5 us (0.982)
  Pallas kernels: 16 us -> 15.7 us
    pallas_call x1, Pallas kernels: 15.1 us -> 14.8 us  [local(): pl.pallas_call(functools.partial(tree_kernel, rows, cols), out_shape=tupl...]
where the time goes in v3:
time: 16.5 us; the launch traced here: 16.4 us
  Pallas kernels  15.7 us (95%)
  between operations  0.64 us (4%)
    pallas_call x1, Pallas kernels, local(): pl.pallas_call(functools.partial(tree_kernel, rows, cols), out_shape=tupl...  14.8 us
    pallas_call x1, Pallas kernels, local(): pl.pallas_call(functools.partial(last_kernel, rows, cols), out_shape=tupl...  0.92 us

profile of v3, /device:TPU:0, one launch (start us, length us, event | category | flops | bytes accessed | tf_op | source)
XLA Modules:
  0.0 16.4 jit_solution(14599933922772935485)
XLA Ops:
  0.6 14.8 %tree.1 = (f32[1024,128]{1,0:T(8,128)S(1)}, f32[2,2,128]{2,1,0:T(2,128)S(1)}, f32[4,4,128]{2,1,0:T(4,128)S(1)}, f32[8,8,128]{2,1,0:T(8,128)S(1)}, f32[14,10,1,12...) custom-call(f32[2,64,128]{2,1,0:T(8,128)} %bitcast.4, ...), custom_call_target="tpu_custom_call" | custom-call | tf_op jit(solution)/shard_map/tree/pallas_call | solution.py:443
  15.5 0.9 %last.1 = (f32[1024,128]{1,0:T(8,128)}, f32[1,1,128]{2,1,0:T(1,128)}, f32[2,2,128]{2,1,0:T(2,128)}, f32[4,4,128]{2,1,0:T(4,128)}, f32[8,8,128]{2,1,0:T(8,128)}, ...) custom-call(f32[1024,128]{1,0:T(8,128)S(1)} %get-tuple-element.22.leaf_ref, f32[2,2,128]{2,1,0:T(2,128)S(1)} %get-tuple-element.23.one_ref, ...), custom_call_target="tpu_custom_call" | custom-call | tf_op jit(solution)/shard_map/last/pallas_call | solution.py:483

commit v4 on v3

--- a/solution.py
+++ b/solution.py
@@ -203,8 +203,7 @@
         load.wait()
 
     def split_weights():
-        for load in loads[3:]:
-            load.wait()
+        loads[3].wait()
         for level in range(shift_ref.shape[0]):
             w_ref[level] = halves(shift_ref[level].reshape(4 * width, width))
 
@@ -222,6 +221,7 @@
     for i, j in others:
         all_copy(i, j, (w, v)).start()
 
+    loads[4].wait()
     l1_ref[...] = jnp.concatenate([level1, jnp.zeros((4, width), F32)], axis=0)
     edge = {-1: 0, 1: 1}
     for dw, dv in AROUND:

time: 16.5 us -> 16.5 us (level)
  no operation moved by 1% of the time
where the time goes in v4:
time: 16.5 us; the launch traced here: 16.4 us
  Pallas kernels  15.7 us (95%)
  between operations  0.64 us (4%)
    pallas_call x1, Pallas kernels, local(): pl.pallas_call(functools.partial(tree_kernel, rows, cols), out_shape=tupl...  14.8 us
    pallas_call x1, Pallas kernels, local(): pl.pallas_call(functools.partial(last_kernel, rows, cols), out_shape=tupl...  0.92 us

profile of v4, /device:TPU:0, one launch (start us, length us, event | category | flops | bytes accessed | tf_op | source)
XLA Modules:
  0.0 16.4 jit_solution(2559888777776447794)
XLA Ops:
  0.6 14.8 %tree.1 = (f32[1024,128]{1,0:T(8,128)S(1)}, f32[2,2,128]{2,1,0:T(2,128)S(1)}, f32[4,4,128]{2,1,0:T(4,128)S(1)}, f32[8,8,128]{2,1,0:T(8,128)S(1)}, f32[14,10,1,12...) custom-call(f32[2,64,128]{2,1,0:T(8,128)} %bitcast.4, ...), custom_call_target="tpu_custom_call" | custom-call | tf_op jit(solution)/shard_map/tree/pallas_call | solution.py:443
  15.5 0.9 %last.1 = (f32[1024,128]{1,0:T(8,128)}, f32[1,1,128]{2,1,0:T(1,128)}, f32[2,2,128]{2,1,0:T(2,128)}, f32[4,4,128]{2,1,0:T(4,128)}, f32[8,8,128]{2,1,0:T(8,128)}, ...) custom-call(f32[1024,128]{1,0:T(8,128)S(1)} %get-tuple-element.22.leaf_ref, f32[2,2,128]{2,1,0:T(2,128)S(1)} %get-tuple-element.23.one_ref, ...), custom_call_target="tpu_custom_call" | custom-call | tf_op jit(solution)/shard_map/last/pallas_call | solution.py:483
